TPU v7x, 256 devices: a whole 4x4x8 slice. The times are simulated.
256 devices in a mesh: dp: 16 (over z_lo, x), mp: 16 (over z_hi, y, core).
Axes of the slice: x: 4, y: 4, z: 8 (z_hi: 2, z_lo: 4; z = z_hi * 4 + z_lo), core: 2. Of those that a mesh axis runs over, the one named last changes fastest.
Arguments:
- teacher_states: bfloat16 [1024, 128, 4096], P('dp', None, 'mp'), may hold values from -6 to 6
- teacher_gain: float32 [4096], P('mp'), may hold values from 0.25 to 1.75
- teacher_proj: bfloat16 [4096, 1024], P('mp'), may hold values from -0.09375 to 0.09375
- teacher_mask: int32 [1024, 128], P('dp'), may hold values 0 or 1
- student_states: bfloat16 [8192, 64, 768], P(('dp', 'mp')), may hold values from -6 to 6
- student_gain: float32 [768], replicated, may hold values from 0.25 to 1.75
- student_proj: bfloat16 [768, 1024], replicated, may hold values from -0.21875 to 0.21875
- student_mask: int32 [8192, 64], P(('dp', 'mp')), may hold values 0 or 1
- positive: int32 [8192], P(('dp', 'mp')), may hold values from 0 to 1023
Outputs:
- grad_embed: float32 [8192, 1024], P(('dp', 'mp'))
- grad_states: bfloat16 [8192, 64, 768], P(('dp', 'mp'))
All inputs are finite; a program needn't handle non-finite values. No bound on the sum of `teacher_mask` or of `student_mask` on one device may be relied on, other than what follows from the above.
Results may differ from a plain program's by a relative error of at most 0.0085.
Values may be sent and summed in bfloat16 or wider, within the bound.
A program may use at most 128 MiB of HBM per device.

v0:
```python
import jax
import jax.numpy as jnp
from jax import lax
from jax.sharding import PartitionSpec as P

D = 4096


def sent_to_all(x, axis):
    copies = jnp.broadcast_to(x, (lax.axis_size(axis), *x.shape))
    return lax.all_to_all(copies, axis, split_axis=0, concat_axis=0, tiled=True)


def of_everyone(x, axis):
    everything = sent_to_all(x, axis)
    return jnp.sum(everything, axis=0)


def total_of_pieces(x, axis):
    parts = lax.all_gather(x, axis)
    return parts.sum(axis=0)


def in_order(parts, dim):
    shape = list(parts.shape[1:])
    shape[dim] *= parts.shape[0]
    return jnp.moveaxis(parts, 0, dim).reshape(shape)


def collect(x, axis, dim):
    return in_order(sent_to_all(x, axis), dim)


def unit_rows(values):
    return (
        values
        * lax.rsqrt(jnp.mean(values * values, axis=-1, keepdims=True) + 1e-06)
        / jnp.sqrt(jnp.float32(values.shape[-1]))
    )


def student_forward(states, gain, proj, live_mask):
    values = states.astype(jnp.float32)
    scale = lax.rsqrt(jnp.mean(values * values, axis=-1, keepdims=True) + 1e-06)
    normed = (values * scale * gain).astype(jnp.bfloat16)
    flat = normed.reshape(-1, normed.shape[-1])
    act = jax.nn.gelu(jnp.dot(flat, proj, preferred_element_type=jnp.float32), approximate=True)
    act = act.reshape(states.shape[0], states.shape[1], -1)
    live = live_mask.astype(jnp.float32)
    pooled = jnp.sum(act * live[:, :, None], axis=1)
    return unit_rows(pooled)


def shards(
    teacher_states,
    teacher_gain,
    teacher_proj,
    teacher_mask,
    student_states,
    student_gain,
    student_proj,
    student_mask,
    positive,
):
    values = teacher_states.astype(jnp.float32)
    partial_squares = jnp.sum(values * values, axis=-1)
    squares = of_everyone(partial_squares, "mp")
    scale = lax.rsqrt(squares / D + 1e-06)
    live = teacher_mask.astype(jnp.float32)
    weight = live * scale
    pooled = jnp.sum(values * weight[:, :, None], axis=1)
    tpooled = (pooled * teacher_gain).astype(jnp.bfloat16)
    partial_embed = jnp.dot(tpooled, teacher_proj, preferred_element_type=jnp.float32)
    summed = total_of_pieces(partial_embed, "mp")
    group_emb = unit_rows(summed).astype(jnp.bfloat16)
    gathered = collect(group_emb, "dp", 0)
    semb, back = jax.vjp(
        lambda st: student_forward(st, student_gain, student_proj, student_mask), student_states
    )
    sround = semb.astype(jnp.bfloat16)
    columns = lax.broadcasted_iota(jnp.int32, (positive.shape[0], gathered.shape[0]), 1)
    picker = (positive[:, None] == columns).astype(jnp.bfloat16)
    tpos = jnp.dot(picker, gathered, preferred_element_type=jnp.float32).astype(jnp.bfloat16)
    tlogit = 10.0 * jnp.dot(tpos, gathered.T, preferred_element_type=jnp.float32)
    slogit = 20.0 * jnp.dot(sround, gathered.T, preferred_element_type=jnp.float32)
    texp = jnp.exp(tlogit)
    sexp = jnp.exp(slogit)
    diff = (
        sexp / jnp.sum(sexp, axis=1, keepdims=True) - texp / jnp.sum(texp, axis=1, keepdims=True)
    ).astype(jnp.bfloat16)
    grad_embed = 20.0 * jnp.dot(diff, gathered, preferred_element_type=jnp.float32)
    grad_states = back(grad_embed)[0]
    return (grad_embed, grad_states)


def solution(mesh):
    in_specs = (
        P("dp", None, "mp"),
        P("mp"),
        P("mp", None),
        P("dp", None),
        P(("dp", "mp"), None, None),
        P(),
        P(),
        P(("dp", "mp"), None),
        P(("dp", "mp")),
    )
    out_specs = (P(("dp", "mp"), None), P(("dp", "mp"), None, None))
    return jax.shard_map(shards, mesh=mesh, in_specs=in_specs, out_specs=out_specs, check_vma=False)
```

profile of v0, /device:TPU:64, one launch (start us, length us, event | category | flops | bytes accessed | tf_op | source)
XLA Modules:
  0.0 221.6 jit_solution(273607529521468672)
XLA Ops:
  7.2 0.0 copy-start
  7.2 0.0 all-gather.3.cloned.1.call-start
  7.3 3.5 %fusion = f32[64,128]{1,0:T(8,128)S(1)} fusion(bf16[64,128,256]{2,1,0:T(8,128)(2,1)} %param.9), kind=kLoop, calls=%fused_computation.9 | loop fusion | flops 6283264 | bytes 4227072 | tf_op jit(solution)/shard_map/reduce_sum | solution.py:66
  10.8 29.6 %all_to_all.10 = f32[16,64,128]{2,1,0:T(8,128)S(1)} all-to-all(f32[16,64,128]{2,1,0:T(8,128)S(1)} %broadcast_in_dim.12), channel_id=1, replica_groups=mesh['dp'=16,'mp'=16] {'mp'}, dimensions={0} | all-to-all | bytes 1048576 | tf_op jit(solution)/shard_map/all_to_all | solution.py:11
  40.4 3.0 %fusion.1 = f32[64,256]{1,0:T(8,128)S(1)} fusion(bf16[64,128,256]{2,1,0:T(8,128)(2,1)} %param.9, f32[64,128]{1,0:T(8,128)S(1)} %rsqrt_multiply_fusion), kind=kLoop, calls=%fused_computation.10 | loop fusion | flops 6275072 | bytes 4292608 | tf_op jit(solution)/shard_map/reduce_sum | solution.py:71
  43.5 0.0 copy-start.6
  43.5 0.9 fusion.36
  44.4 0.0 all-gather.3.cloned.1.call-update
  44.4 71.4 %all-gather.3.cloned.1.call-done = f32[1024,1024]{1,0:T(8,128)} async-done(((f32[64,1024]{1,0:T(8,128)}), f32[1024,1024]{1,0:T(8,128)}) %all-gather.3.cloned.1.call-update) | async-done | bytes 4194320 | tf_op jit(solution)/shard_map/all_gather | solution.py:20
  115.9 2.5 %reduce_sum.122 = f32[64,1024]{1,0:T(8,128)S(1)} reduce(f32[16,64,1024]{2,1,0:T(8,128)} %bitcast.34, f32[]{:T(128)} %constant.16.clone.1), dimensions={0}, to_apply=%region_6.0 | reduce | flops 983040 | bytes 4456452 | tf_op jit(solution)/shard_map/reduce_sum | solution.py:21
  118.4 0.1 multiply_reduce_fusion.1
  118.5 0.1 multiply_convert_fusion
  118.6 1.6 broadcast_in_dim.13
  120.2 6.7 %all-to-all-start.1 = ((bf16[16,64,1024]{2,1,0:T(8,128)(2,1)}), bf16[16,64,1024]{2,1,0:T(8,128)(2,1)}, u32[]{:S(2)}, u32[]{:S(2)}) async-start(bf16[16,64,1024]{2,1,0:T(8,128)(2,1)} %broadcast_in_dim.13), calls=%async_computation.1 | async-start | bytes 4194304 | tf_op jit(solution)/shard_map/all_to_all | solution.py:11
  126.8 0.0 copy-done.6
  126.9 0.1 mul.242
  126.9 2.6 %fusion.17 = f32[32,64]{1,0:T(8,128)S(1)} fusion(bf16[32,64,768]{2,1,0:T(8,128)(2,1)} %param.13), kind=kLoop, calls=%fused_computation.28 | loop fusion | flops 4716544 | bytes 3153920 | tf_op jit(solution)/shard_map/jvp()/reduce_sum | solution.py:44
  129.5 2.7 %fusion.19 = bf16[32,64,768]{2,1,0:T(8,128)(2,1)S(1)} fusion(bf16[32,64,768]{2,1,0:T(8,128)(2,1)} %param.13, f32[768]{0:T(1024)S(1)} %copy-done.4, f32[32,64]{1,0:T(8,128)S(1)} %fusion.38), kind=kLoop, calls=%fused_computation.30 | loop fusion | flops 6291456 | bytes 6302720 | tf_op jit(solution)/shard_map/jvp()/convert_element_type | solution.py:45
  132.2 0.0 copy-start.8
  132.2 7.5 %multiply_reduce_fusion = (f32[32,1024]{1,0:T(8,128)S(1)}, f32[2048,1024]{1,0:T(8,128)}) fusion(f32[32,64]{1,0:T(8,128)S(1)} %convert_element_type.45, bf16[2048,768]{1,0:T(8,128)(2,1)S(1)} %bitcast.33, bf16[768,1024]{1,0:T(8,128)(2,1)S(1)} %copy-done), kind=kOutput, calls=%fused_computation.25 | convolution fusion | flops 3242164224 | bytes 13246464 | tf_op jit(solution)/shard_map/jvp()/dot_general | solution.py:47
  139.7 0.1 multiply_reduce_fusion.3
  139.9 35.8 %all-to-all-done.1 = bf16[16,64,1024]{2,1,0:T(8,128)(2,1)} async-done(((bf16[16,64,1024]{2,1,0:T(8,128)(2,1)}), bf16[16,64,1024]{2,1,0:T(8,128)(2,1)}, u32[]{:S(2)}, u32[]{:S(2)}) %all-to-all-start.1) | async-done | bytes 2097184 | tf_op jit(solution)/shard_map/all_to_all | solution.py:11
  175.6 3.5 %fusion.43 = (f32[32]{0:T(128)S(1)}, f32[32,1024]{1,0:T(8,128)S(1)}) fusion(bf16[1024,1024]{1,0:T(8,128)(2,1)} %bitcast.3, s32[32]{0:T(128)S(1)} %copy-done.8), kind=kOutput, calls=%fused_computation.72 | convolution fusion | flops 134348768 | bytes 2228480 | tf_op jit(solution)/shard_map/dot_general | solution.py:84
  179.2 2.5 %fusion.44 = (f32[32]{0:T(128)S(1)}, f32[32,1024]{1,0:T(8,128)S(1)}) fusion(bf16[1024,1024]{1,0:T(8,128)(2,1)} %bitcast.3, f32[32,1024]{1,0:T(8,128)S(1)} %get-tuple-element.8, f32[32]{0:T(128)S(1)} %fusion.39), kind=kOutput, calls=%fused_computation.73 | convolution fusion | flops 67272672 | bytes 2359552 | tf_op jit(solution)/shard_map/dot_general | solution.py:85
  181.6 2.2 %multiply_reduce_fusion.2 = (f32[32]{0:T(128)S(1)}, f32[32,1024]{1,0:T(8,128)S(1)}) fusion(f32[32,1024]{1,0:T(8,128)S(1)} %get-tuple-element.8, bf16[1024,1024]{1,0:T(8,128)(2,1)} %bitcast.3, f32[32,1024]{1,0:T(8,128)S(1)} %get-tuple-element.11, f32[32,1024]{1,0:T(8,128)S(1)} %get-tuple-element.13, f32[32]{0:T(128)S(1)} %get-tuple-element.10, ...), kind=kOutput, calls=%fused_computation.45 | convolution fusion | flops 67338208 | bytes 2621824 | tf_op jit(solution)/shard_map/dot_general | solution.py:91
  183.9 0.0 slice-start
  183.9 0.7 add_add_fusion.1
  184.5 11.1 %fusion.14 = (f32[2048,1024]{1,0:T(8,128)}, f32[2048,1024]{1,0:T(8,128)}) fusion(f32[2048,1024]{1,0:T(8,128)} %get-tuple-element.9, f32[2048]{0:T(1024)S(1)} %mul.242, f32[32,1024]{1,0:T(8,128)S(1)} %get-tuple-element.4), kind=kLoop, calls=%fused_computation.23 | loop fusion | flops 33554432 | bytes 25305088 | tf_op jit(solution)/shard_map/transpose(jvp())/mul | solution.py:47
  195.6 11.6 %fusion.24 = bf16[2048,768]{1,0:T(8,128)(2,1)} fusion(bf16[768,1024]{1,0:T(8,128)(2,1)S(1)} %copy-done, f32[2048,1024]{1,0:T(8,128)} %get-tuple-element.3, f32[2048,1024]{1,0:T(8,128)S(1)} %bitcast.31, f32[2048,1024]{1,0:T(8,128)} %get-tuple-element.2), kind=kOutput, calls=%fused_computation.36 | convolution fusion | flops 3233284096 | bytes 29884416 | tf_op jit(solution)/shard_map/transpose(jvp())/dot_general | solution.py:47
  207.3 4.1 %fusion.20 = f32[32,64]{1,0:T(8,128)S(1)} fusion(bf16[32,64,768]{2,1,0:T(8,128)(2,1)} %param.13, bf16[32,64,768]{2,1,0:T(8,128)(2,1)} %bitcast.32, f32[768]{0:T(1024)S(1)} %copy-done.4), kind=kLoop, calls=%fused_computation.31 | loop fusion | flops 7862272 | bytes 6302720 | tf_op jit(solution)/shard_map/transpose(jvp())/reduce_sum | solution.py:45
  211.4 0.6 copy-done.2
  212.0 2.8 %fusion.16 = bf16[32,64,768]{2,1,0:T(8,128)(2,1)} fusion(bf16[32,64,768]{2,1,0:T(8,128)(2,1)S(1)} %copy-done.1, f32[32,64]{1,0:T(8,128)S(1)} %multiply_multiply_fusion.3, f32[768]{0:T(1024)S(1)} %copy-done.4, f32[32,64]{1,0:T(8,128)S(1)} %fusion.38, bf16[2048,768]{1,0:T(8,128)(2,1)S(1)} %copy-done.2), kind=kLoop, calls=%fused_computation.27 | loop fusion | flops 12582912 | bytes 9456640 | tf_op jit(solution)/shard_map/transpose(jvp())/convert_element_type | solution.py:43
  (26 shorter events, 0.2 us)
Async XLA Ops:
  7.2 125.0 %copy-start = (bf16[768,1024]{1,0:T(8,128)(2,1)S(1)}, bf16[768,1024]{1,0:T(8,128)(2,1)}, u32[]{:S(2)}) copy-start(bf16[768,1024]{1,0:T(8,128)(2,1)} %param.15) | copy-start | bytes 4718596
  7.2 33.2 %copy-start.5 = (s32[64,128]{1,0:T(8,128)S(1)}, s32[64,128]{1,0:T(8,128)}, u32[]{:S(2)}) copy-start(s32[64,128]{1,0:T(8,128)} %param.12) | copy-start | bytes 98308
  7.2 36.3 %copy-start.3 = (bf16[256,1024]{1,0:T(8,128)(2,1)S(1)}, bf16[256,1024]{1,0:T(8,128)(2,1)}, u32[]{:S(2)}) copy-start(bf16[256,1024]{1,0:T(8,128)(2,1)} %param.11) | copy-start | bytes 1572868
  7.2 36.3 %copy-start.7 = (f32[256]{0:T(256)S(1)}, f32[256]{0:T(256)}, u32[]{:S(2)}) copy-start(f32[256]{0:T(256)} %param.10) | copy-start | bytes 3076
  7.2 108.7 %all-gather.3.cloned.1.call-start = ((), (), s32[]{:S(2)}) async-start(), calls=%async_computation.2 | async-start | bytes 4456448 | tf_op jit(solution)/shard_map/all_gather | solution.py:20
  43.5 83.4 %copy-start.6 = (s32[32,64]{1,0:T(8,128)S(1)}, s32[32,64]{1,0:T(8,128)}, u32[]{:S(2)}) copy-start(s32[32,64]{1,0:T(8,128)} %param.16) | copy-start | bytes 24580
  115.9 13.6 %copy-start.4 = (f32[768]{0:T(1024)S(1)}, f32[768]{0:T(1024)}, u32[]{:S(2)}) copy-start(f32[768]{0:T(1024)} %param.14) | copy-start | bytes 9220
  120.2 55.5 %all-to-all-start.1 = ((bf16[16,64,1024]{2,1,0:T(8,128)(2,1)}), bf16[16,64,1024]{2,1,0:T(8,128)(2,1)}, u32[]{:S(2)}, u32[]{:S(2)}) async-start(bf16[16,64,1024]{2,1,0:T(8,128)(2,1)} %broadcast_in_dim.13), calls=%async_computation.1 | async-start | bytes 4194304 | tf_op jit(solution)/shard_map/all_to_all | solution.py:11
  132.2 43.4 %copy-start.8 = (s32[32]{0:T(128)S(1)}, s32[32]{0:T(128)}, u32[]{:S(2)}) copy-start(s32[32]{0:T(128)} %param.17) | copy-start | bytes 388
  183.9 11.8 %slice-start = ((s8[8388608]{0:T(1024)(128)(4,1)}), s8[4194304]{0:T(1024)(128)(4,1)S(1)}, s32[]{:S(2)}) async-start(s8[8388608]{0:T(1024)(128)(4,1)} %bitcast.30), calls=%async_computation.3 | async-start | bytes 8388608
  184.5 11.1 %slice-start.1 = ((s8[8388608]{0:T(1024)(128)(4,1)}), s8[4194304]{0:T(1024)(128)(4,1)S(1)}, s32[]{:S(2)}) async-start(s8[8388608]{0:T(1024)(128)(4,1)} %bitcast.30), calls=%async_computation.4 | async-start | bytes 8388608
  207.3 4.1 %copy-start.1 = (bf16[32,64,768]{2,1,0:T(8,128)(2,1)S(1)}, bf16[32,64,768]{2,1,0:T(8,128)(2,1)}, u32[]{:S(2)}) copy-start(bf16[32,64,768]{2,1,0:T(8,128)(2,1)} %param.13) | copy-start | bytes 9437188
  207.3 4.7 %copy-start.2 = (bf16[2048,768]{1,0:T(8,128)(2,1)S(1)}, bf16[2048,768]{1,0:T(8,128)(2,1)}, u32[]{:S(2)}) copy-start(bf16[2048,768]{1,0:T(8,128)(2,1)} %fusion.24) | copy-start | bytes 9437188
Sparse Core Ops, SparseCore 0:
  44.6 71.2 all-gather.2
where the time goes:
time: 222 us
  waiting for transfers between devices  107 us (48%)
  other arithmetic  33.3 us (15%)
  blocking collectives  29.6 us (13%)
  matrix products  28.3 us (13%)
  between operations  14.2 us (6%)
  starting transfers between devices  6.7 us (3%)
  local copies, waits for them, and re-layouts  2.35 us (1%)
    all_gather x1, waiting for transfers between devices, total_of_pieces(): parts = lax.all_gather(x, axis)  71.4 us
    all_to_all x1, waiting for transfers between devices, sent_to_all(): return lax.all_to_all(copies, axis, split_axis=0, concat_axis=0, tiled=True)  35.8 us
    all_to_all x1, blocking collectives, sent_to_all(): return lax.all_to_all(copies, axis, split_axis=0, concat_axis=0, tiled=True)  29.6 us
    dot_general x2, matrix products, student_forward(): jnp.dot(flat, proj, preferred_element_type=jnp.float32)  19.2 us
    mul x1, other arithmetic, student_forward(): jax.nn.gelu(jnp.dot(flat, proj, preferred_element_type=jnp.float32), appr...  11.1 us
    all_to_all x1, starting transfers between devices, sent_to_all(): return lax.all_to_all(copies, axis, split_axis=0, concat_axis=0, tiled=True)  6.66 us
  transfers between devices with their start and end apart: 2, of which 2 were waited for; matrix products, arithmetic and copies ran while one was open for 6% of the time, Pallas kernels for 0%

commit v1 on v0

v1 whole, which is shorter than its diff:
```python
import functools

import jax
import jax.numpy as jnp
from jax import lax
from jax.experimental import pallas as pl
from jax.experimental.pallas import tpu as pltpu
from jax.sharding import PartitionSpec as P

D = 4096
F32 = jnp.float32
BF16 = jnp.bfloat16
MESH = pl.DeviceIdType.MESH
NT = (((1,), (1,)), ((), ()))
PARTS = ((0, 384), (384, 384), (768, 256))
GELU_C = 0.7978845608028654
GELU_K = 0.044715


def place():
    d, m = lax.axis_index("dp"), lax.axis_index("mp")
    return lax.div(d, 4), lax.rem(d, 4), lax.div(m, 8), lax.rem(lax.div(m, 2), 4), lax.rem(m, 2)


def student_chunk(i, sx, sproj, sgain, live, gp, praw, sl_out, normed):
    rows = pl.ds(i * 512, 512)
    x = sx[rows, :].astype(F32)
    scale = lax.rsqrt(jnp.sum(x * x, axis=1, keepdims=True) / 768.0 + 1e-06)
    sl = scale * live[:, i : i + 1]
    sl_out[rows, :] = jnp.broadcast_to(sl, (512, 128))
    normed[...] = (x * sl * sgain[...]).astype(BF16)

    def block(n, carry):
        cols = pl.ds(pl.multiple_of(n * 256, 256), 256)
        pre = jnp.dot(normed[...], sproj[:, cols], preferred_element_type=F32)
        sq = pre * pre
        half = 0.5 + 0.5 * jnp.tanh(pre * (GELU_C + (GELU_C * GELU_K) * sq))
        act = pre * half
        gp[rows, cols] = (
            half + act * (1.0 - half) * (2.0 * GELU_C + (6.0 * GELU_C * GELU_K) * sq)
        ).astype(BF16)
        praw[i * 8 : i * 8 + 8, cols] = jnp.sum(act.reshape(8, 64, 256), axis=1)
        return carry

    lax.fori_loop(0, 4, block, 0)


def gather_kernel(
    tx_hbm, tproj_hbm, tgain, tlive, sx_hbm, sproj_hbm, sgain, slive, pos,
    ge, gp, praw, sl_out,
    tx, tproj, sx, sproj, normed,
    sq_own, sq_out, sq_in, sqz_out, sqz_in,
    pe_own, pe_out, pe_in, pez_out, pez_in, T,
    ld_sem, sq_s, sq_r, pe_s, pe_r, z_s, z_r, a1_s, a1_r, a2_s, a2_r, c_s, c_r,
):
    zlo, x, zhi, y, core = place()
    z = zhi * 4 + zlo
    two = 2 - 4 * core

    def dev(zz, xx, yy, cc):
        zz, xx, yy = lax.rem(zz + 8, 8), lax.rem(xx + 4, 4), lax.rem(yy + 4, 4)
        return {"dp": lax.rem(zz, 4) * 4 + xx, "mp": lax.div(zz, 4) * 8 + yy * 2 + cc}

    loads = []
    for k in range(4):
        loads.append(pltpu.make_async_copy(tx_hbm.at[pl.ds(16 * k, 16)], tx.at[pl.ds(16 * k, 16)], ld_sem.at[k]))
    loads.append(pltpu.make_async_copy(sx_hbm, sx, ld_sem.at[4]))
    loads.append(pltpu.make_async_copy(sproj_hbm, sproj, ld_sem.at[5]))
    loads.append(pltpu.make_async_copy(tproj_hbm, tproj, ld_sem.at[6]))
    for c in loads:
        c.start()

    peers = []
    for dz in (0, 1, -1, 2, -2):
        for dy in range(4):
            if (dz, dy) != (0, 0):
                peers.append(dev(z + dz, x, y + dy, core))
        for dx in range(1, 4):
            peers.append(dev(z + dz, x + dx, y, core))
    for dx in range(1, 4):
        for dy in range(1, 4):
            peers.append(dev(z, x + dx, y + dy, core))
    for dy in range(4):
        peers.append(dev(z, x, y + dy, 1 - core))
    peers.append(dev(z + 4, x, y, core))
    barrier = pltpu.get_barrier_semaphore()
    for p in peers:
        pl.semaphore_signal(barrier, inc=1, device_id=p, device_id_type=MESH)

    def remote(src, dst, ss, rs, to):
        return pltpu.make_async_remote_copy(
            src_ref=src, dst_ref=dst, send_sem=ss, recv_sem=rs, device_id=to, device_id_type=MESH
        )

    me = y * 2 + core
    others = [lax.rem(me + k, 8) for k in range(1, 8)]
    sends = []

    def peer8(s):
        return dev(z, x, lax.div(s, 2), lax.rem(s, 2))

    row = lax.broadcasted_iota(jnp.int32, (16, 256), 0)
    for h in range(2):
        total = jnp.zeros((16, 256), F32)
        for q in range(16):
            if q % 8 == 0:
                loads[2 * h + q // 8].wait()
            p = 32 * h + 2 * q
            v = tx[p : p + 2].reshape(256, 256)
            pick = jnp.where(row == q, 1.0, 0.0).astype(BF16)
            total = total + lax.dot_general(pick, v * v, NT, preferred_element_type=F32)
        sq_own[h] = total
        sq_out[h] = total.astype(BF16)
        if h == 0:
            pl.semaphore_wait(barrier, len(peers))
        for s in others:
            c = remote(sq_out.at[h], sq_in.at[h, me], sq_s.at[h, s], sq_r.at[h, me], peer8(s))
            c.start()
            sends.append(c)

    loads[4].wait()
    loads[5].wait()
    student = functools.partial(
        student_chunk, sx=sx, sproj=sproj, sgain=sgain, live=slive, gp=gp, praw=praw, sl_out=sl_out, normed=normed
    )
    student(0)

    partner = dev(z + 4, x, y, core)
    for h in range(2):
        for s in others:
            remote(sq_in.at[h, s], sq_in.at[h, s], sq_s.at[h, s], sq_r.at[h, s], partner).wait_recv()
        total = sq_own[h]
        for s in others:
            total = total + sq_in[h, s].astype(F32)
        sq_own[h] = total
        sqz_out[h] = total.astype(BF16)
    zc = remote(sqz_out, sqz_in, z_s.at[0], z_r.at[0], partner)
    zc.start()
    sends.append(zc)
    student(1)
    zc.wait_recv()

    loads[6].wait()
    row = lax.broadcasted_iota(jnp.int32, (16, 256), 0)
    lane = lax.broadcasted_iota(jnp.int32, (16, 256), 1)
    pooled = []
    for h in range(2):
        squares = sq_own[h] + sqz_in[h].astype(F32)
        weight = tlive[16 * h : 16 * h + 16, :] * lax.rsqrt(squares / D + 1e-06)
        high = weight.astype(BF16).astype(F32)
        low = weight - high
        for g in range(4):
            total = jnp.zeros((16, 256), F32)
            for k in range(4):
                q = 4 * g + k
                both = jnp.where(row < 8, high[q : q + 1, :], low[q : q + 1, :])
                mine = lax.rem(row, 8) == 2 * k + lax.div(lane, 128)
                lhs = jnp.where(mine, both, 0.0).astype(BF16)
                p = 32 * h + 2 * q
                v = tx[p : p + 2].reshape(256, 256)
                total = total + jnp.dot(lhs, v, preferred_element_type=F32)
            pooled.append(total[:8] + total[8:])
    tpooled = (jnp.concatenate(pooled, axis=0) * tgain[...]).astype(BF16)
    partial = jnp.dot(tpooled, tproj[...], preferred_element_type=F32).reshape(8, 8, 1024)
    pe_own[...] = partial
    pe_out[...] = partial.astype(BF16)
    for s in others:
        c = remote(pe_out.at[s], pe_in.at[me], pe_s.at[s], pe_r.at[me], peer8(s))
        c.start()
        sends.append(c)
    student(2)
    for s in others:
        remote(pe_in.at[s], pe_in.at[s], pe_s.at[s], pe_r.at[s], partner).wait_recv()
    total = pe_own[me]
    for s in others:
        total = total + pe_in[s].astype(F32)
    pez_out[...] = total.astype(BF16)
    zc = remote(pez_out, pez_in, z_s.at[1], z_r.at[1], partner)
    zc.start()
    sends.append(zc)
    student(3)
    zc.wait_recv()
    traw = total + pez_in[...].astype(F32)
    scale = lax.rsqrt(jnp.mean(traw * traw, axis=-1, keepdims=True) + 1e-06)
    T[core, zlo, x, y] = (traw * scale / 32.0).astype(BF16)

    zoffs = (0, 1, -1, two)
    ahead = lambda v, k: lax.rem(v + k, 4)

    def plane(part, az, ax, ay):
        lo, n = PARTS[part]
        return T.at[core, az, ax, ay, :, pl.ds(lo, n)]

    slots = (zlo * 4 + y, zlo * 4 + x, x * 4 + y)
    for part in range(3):
        mine = plane(part, zlo, x, y)
        targets = []
        if part == 0:
            targets = [dev(z + zoffs[a], x, y + b, core) for a in range(4) for b in range(4) if a or b]
        elif part == 1:
            targets = [dev(z + zoffs[a], x + b, y, core) for a in range(4) for b in range(4) if a or b]
        else:
            targets = [dev(z, x + a, y + b, core) for a in range(4) for b in range(4) if a or b]
        for k, to in enumerate(targets):
            c = remote(mine, mine, a1_s.at[part, k], a1_r.at[part, slots[part]], to)
            c.start()
            sends.append(c)

    def line(part, cc, v):
        lo, n = PARTS[part]
        cols = pl.ds(lo, n)
        if part == 0:
            return T.at[cc, :, v, :, :, cols]
        if part == 1:
            return T.at[cc, :, :, v, :, cols]
        return T.at[cc, v, :, :, :, cols]

    own_line = (x, y, zlo)
    other = dev(z, x, y, 1 - core)
    for part in range(3):
        mine = plane(part, zlo, x, y)
        for k in range(1, 16):
            s = lax.rem(slots[part] + k, 16)
            remote(mine, mine, a1_s.at[part, k - 1], a1_r.at[part, s], other).wait_recv()
        v = own_line[part]
        src = line(part, core, v)
        if part == 0:
            targets = [dev(z, x + k, y, core) for k in (1, 3, 2)]
        elif part == 1:
            targets = [dev(z, x, y + k, core) for k in (1, 3, 2)]
        else:
            targets = [dev(z + zoffs[k], x, y, core) for k in (1, 2, 3)]
        for k, to in enumerate(targets):
            c = remote(src, src, a2_s.at[part, k], a2_r.at[part, v], to)
            c.start()
            sends.append(c)
        c = remote(src, src, c_s.at[part, v], c_r.at[part, v], other)
        c.start()
        sends.append(c)
    for k in (1, 3, 2):
        for part in range(3):
            v = ahead(own_line[part], k)
            src = line(part, core, v)
            remote(src, src, a2_s.at[part, 0], a2_r.at[part, v], other).wait_recv()
            c = remote(src, src, c_s.at[part, v], c_r.at[part, v], other)
            c.start()
            sends.append(c)
    for part in range(3):
        for v in range(4):
            dst = line(part, 1 - core, v)
            remote(dst, dst, c_s.at[part, v], c_r.at[part, v], other).wait_recv()

    praws = praw[...]
    semb = praws * lax.rsqrt(jnp.mean(praws * praws, axis=-1, keepdims=True) + 1e-06) / 32.0
    temb = T[...].reshape(1024, 1024)
    lanes = lax.broadcasted_iota(jnp.int32, (32, 1024), 1)
    picker = jnp.where(pos[...] == lanes, 1.0, 0.0).astype(BF16)
    tpos = jnp.dot(picker, temb, preferred_element_type=F32).astype(BF16)
    both = jnp.concatenate([tpos, semb.astype(BF16)], axis=0)
    logits = lax.dot_general(both, temb, NT, preferred_element_type=F32)
    texp = jnp.exp(10.0 * logits[:32])
    sexp = jnp.exp(20.0 * logits[32:])
    diff = sexp / jnp.sum(sexp, axis=1, keepdims=True) - texp / jnp.sum(texp, axis=1, keepdims=True)
    ge[...] = 20.0 * jnp.dot(diff.astype(BF16), temb, preferred_element_type=F32)

    for c in sends:
        c.wait_send()


def back_kernel(ge, praw, gp, sl_in, sproj, sgain, sx, ge_hbm, out_hbm, out, st_sem):
    stores = [pltpu.make_async_copy(ge, ge_hbm, st_sem.at[8])]
    stores[0].start()
    p, g = praw[...], ge[...]
    r = lax.rsqrt(jnp.mean(p * p, axis=-1, keepdims=True) + 1e-06)
    ds = (g * r - p * (r * r * r) * jnp.mean(p * g, axis=-1, keepdims=True)) / 32.0
    gain = sgain[...]
    for i in range(8):
        rows = pl.ds(256 * i, 256)
        slope = gp[rows, :].astype(F32).reshape(4, 64, 1024)
        dpre = (slope * ds[4 * i : 4 * i + 4][:, None, :]).reshape(256, 1024).astype(BF16)
        dn = lax.dot_general(dpre, sproj[...], NT, preferred_element_type=F32)
        dy = dn.astype(BF16).astype(F32) * gain
        x = sx[rows, :].astype(F32)
        sl = sl_in[rows, :1]
        m = jnp.sum(x * dy, axis=1, keepdims=True) * (sl * sl / 768.0)
        out[rows, :] = (sl * (dy - x * m)).astype(BF16)
        stores.append(pltpu.make_async_copy(out.at[rows], out_hbm.at[rows], st_sem.at[i]))
        stores[-1].start()
    for c in stores:
        c.wait()


def shards(
    teacher_states, teacher_gain, teacher_proj, teacher_mask,
    student_states, student_gain, student_proj, student_mask, positive,
):
    vmem = pl.BlockSpec(memory_space=pltpu.VMEM)
    hbm = pl.BlockSpec(memory_space=pltpu.HBM)
    dma = pltpu.SemaphoreType.DMA
    in_hbm = lambda a: pltpu.with_memory_space_constraint(a, pltpu.HBM)
    sx = student_states.reshape(2048, 768)
    sgain = student_gain.reshape(1, 768)
    slive = student_mask.astype(F32).reshape(4, 512).T
    tlive = teacher_mask.astype(F32).reshape(32, 256)
    p = positive
    pos = ((p // 8) % 2) * 512 + (p // 256) * 128 + ((p // 64) % 4) * 32 + ((p // 16) % 4) * 8 + p % 8
    ge, gp, praw, sl = pl.pallas_call(
        gather_kernel,
        name="gather",
        out_shape=(
            jax.ShapeDtypeStruct((32, 1024), F32),
            jax.ShapeDtypeStruct((2048, 1024), BF16),
            jax.ShapeDtypeStruct((32, 1024), F32),
            jax.ShapeDtypeStruct((2048, 128), F32),
        ),
        in_specs=[hbm, hbm, vmem, vmem, hbm, hbm, vmem, vmem, vmem],
        out_specs=(vmem, vmem, vmem, vmem),
        scratch_shapes=[
            pltpu.VMEM((64, 128, 256), BF16),
            pltpu.VMEM((256, 1024), BF16),
            pltpu.VMEM((2048, 768), BF16),
            pltpu.VMEM((768, 1024), BF16),
            pltpu.VMEM((512, 768), BF16),
            pltpu.VMEM((2, 16, 256), F32),
            pltpu.VMEM((2, 16, 256), BF16),
            pltpu.VMEM((2, 8, 16, 256), BF16),
            pltpu.VMEM((2, 16, 256), BF16),
            pltpu.VMEM((2, 16, 256), BF16),
            pltpu.VMEM((8, 8, 1024), F32),
            pltpu.VMEM((8, 8, 1024), BF16),
            pltpu.VMEM((8, 8, 1024), BF16),
            pltpu.VMEM((8, 1024), BF16),
            pltpu.VMEM((8, 1024), BF16),
            pltpu.VMEM((2, 4, 4, 4, 8, 1024), BF16),
            dma((7,)), dma((2, 8)), dma((2, 8)), dma((8,)), dma((8,)), dma((2,)), dma((2,)),
            dma((3, 15)), dma((3, 16)), dma((3, 3)), dma((3, 4)), dma((3, 4)), dma((3, 4)),
        ],
        compiler_params=pltpu.CompilerParams(
            collective_id=0, has_side_effects=True, vmem_limit_bytes=36 * 2**20
        ),
    )(
        in_hbm(teacher_states), in_hbm(teacher_proj), teacher_gain.reshape(1, 256), tlive,
        in_hbm(sx), in_hbm(student_proj), sgain, slive, pos.reshape(32, 1),
    )
    grad_embed, grad_states = pl.pallas_call(
        back_kernel,
        name="back",
        out_shape=(jax.ShapeDtypeStruct((32, 1024), F32), jax.ShapeDtypeStruct((2048, 768), BF16)),
        in_specs=[vmem] * 7,
        out_specs=(hbm, hbm),
        scratch_shapes=[pltpu.VMEM((2048, 768), BF16), dma((9,))],
        compiler_params=pltpu.CompilerParams(vmem_limit_bytes=36 * 2**20),
    )(ge, praw, gp, sl, student_proj, sgain, sx)
    return grad_embed, grad_states.reshape(32, 64, 768)


def solution(mesh):
    in_specs = (
        P("dp", None, "mp"), P("mp"), P("mp", None), P("dp", None),
        P(("dp", "mp"), None, None), P(), P(), P(("dp", "mp"), None), P(("dp", "mp")),
    )
    out_specs = (P(("dp", "mp"), None), P(("dp", "mp"), None, None))
    return jax.shard_map(shards, mesh=mesh, in_specs=in_specs, out_specs=out_specs, check_vma=False)
```

time: 222 us -> 56.8 us (0.26)
  the two profiles are of different devices: /device:TPU:64 before, /device:TPU:1 now
where the time goes in v1:
time: 56.8 us; the launch traced here: 56.6 us
  Pallas kernels  52 us (92%)
  other arithmetic  2.16 us (4%)
  local copies, waits for them, and re-layouts  1.7 us (3%)
  between operations  0.68 us (1%)
    pallas_call x1, Pallas kernels, shards(): pl.pallas_call(gather_kernel, name='gather', out_shape=(jax.ShapeDtypeStr...  46.1 us
    pallas_call x1, Pallas kernels, shards(): pl.pallas_call(back_kernel, name='back', out_shape=(jax.ShapeDtypeStruct(...  5.93 us

profile of v1, /device:TPU:1, one launch (start us, length us, event | category | flops | bytes accessed | tf_op | source)
XLA Modules:
  0.0 56.6 jit_solution(3165412017597371945)
XLA Ops:
  0.6 0.7 %fusion.10 = s32[32,1]{0,1:T(1,128)S(1)} fusion(s32[32]{0:T(128)} %param.17), kind=kLoop, calls=%fused_computation.33 | loop fusion | flops 2880 | bytes 256 | tf_op jit(solution)/shard_map/reshape | solution.py:343
  1.3 0.7 %reshape.28.sgain = f32[1,768]{1,0:T(1,128)S(1)} reshape(f32[768]{0:T(1024)} %param.14) | data formatting | bytes 6144 | tf_op jit(solution)/shard_map/reshape | solution.py:302
  2.0 0.1 copy.13.pos
  2.1 0.7 %convert_element_type.7 = f32[32,64]{1,0:T(8,128)S(1)} convert(s32[32,64]{1,0:T(8,128)} %param.16) | non-fusion elementwise | flops 2048 | bytes 16384 | tf_op jit(solution)/shard_map/convert_element_type | solution.py:303
  2.8 0.1 reshape.29
  2.9 0.8 %convert_element_type.6 = f32[64,128]{1,0:T(8,128)S(1)} convert(s32[64,128]{1,0:T(8,128)} %param.12) | non-fusion elementwise | flops 8192 | bytes 65536 | tf_op jit(solution)/shard_map/convert_element_type | solution.py:304
  3.7 0.1 copy.12
  3.8 0.0 copy-start.2
  3.8 0.7 %copy-done.2 = f32[256]{0:T(256)S(1)} copy-done((f32[256]{0:T(256)S(1)}, f32[256]{0:T(256)}, u32[]{:S(2)}) %copy-start.2) | copy-done | bytes 1048
  4.5 0.0 copy-start
  4.5 0.0 copy-start.1
  4.5 46.1 %gather.1 = (f32[32,1024]{1,0:T(8,128)S(1)}, bf16[2048,1024]{1,0:T(8,128)(2,1)S(1)}, f32[32,1024]{1,0:T(8,128)S(1)}, f32[2048,128]{1,0:T(8,128)S(1)}) custom-call(bf16[64,128,256]{2,1,0:T(8,128)(2,1)} %tx_hbm.1, bf16[256,1024]{1,0:T(8,128)(2,1)} %tproj_hbm.1, f32[1,256]{1,0:T(1,128)S(1)} %bitcast.9, f32[32,256]{1,0:T(8,128)S(1)} %reshape.26.tlive, ...), custom_call_target="tpu_custom_call" | custom-call | tf_op jit(solution)/shard_map/gather/pallas_call | solution.py:307
  50.6 0.0 copy-done
  50.6 0.0 copy-done.1
  50.6 5.9 %back.1 = (f32[32,1024]{1,0:T(8,128)}, bf16[2048,768]{1,0:T(8,128)(2,1)}) custom-call(f32[32,1024]{1,0:T(8,128)S(1)} %get-tuple-element.8.ge, f32[32,1024]{1,0:T(8,128)S(1)} %get-tuple-element.9.praw, bf16[2048,1024]{1,0:T(8,128)(2,1)S(1)} %get-tuple-element.10.gp, f32[2048,128]{1,0:T(8,128)S(1)} %get-tuple-element.11.sl_in, ...), custom_call_target="tpu_custom_call" | custom-call | tf_op jit(solution)/shard_map/back/pallas_call | solution.py:345
  (1 shorter events, 0.0 us)
Async XLA Ops:
  3.8 0.7 %copy-start.2 = (f32[256]{0:T(256)S(1)}, f32[256]{0:T(256)}, u32[]{:S(2)}) copy-start(f32[256]{0:T(256)} %param.10) | copy-start | bytes 3076
  4.5 46.1 %copy-start = (bf16[32,64,768]{2,1,0:T(8,128)(2,1)S(1)}, bf16[32,64,768]{2,1,0:T(8,128)(2,1)}, u32[]{:S(2)}) copy-start(bf16[32,64,768]{2,1,0:T(8,128)(2,1)} %param.13) | copy-start | bytes 9437188
  4.5 46.1 %copy-start.1 = (bf16[768,1024]{1,0:T(8,128)(2,1)S(1)}, bf16[768,1024]{1,0:T(8,128)(2,1)}, u32[]{:S(2)}) copy-start(bf16[768,1024]{1,0:T(8,128)(2,1)} %sproj.1) | copy-start | bytes 4718596

commit v2 on v1

--- a/solution.py
+++ b/solution.py
@@ -19,16 +19,20 @@
 
 def place():
     d, m = lax.axis_index("dp"), lax.axis_index("mp")
-    return lax.div(d, 4), lax.rem(d, 4), lax.div(m, 8), lax.rem(lax.div(m, 2), 4), lax.rem(m, 2)
-
-
-def student_chunk(i, sx, sproj, sgain, live, gp, praw, sl_out, normed):
+    return d >> 2, d & 3, m >> 3, (m >> 1) & 3, m & 1
+
+
+def student_chunk(i, sx, sproj, sgain, mask, gp, praw, sl_out, normed):
     rows = pl.ds(i * 512, 512)
+    diagonal = lax.broadcasted_iota(jnp.int32, (64, 64), 0) == lax.broadcasted_iota(jnp.int32, (64, 64), 1)
+    live = mask[8 * i : 8 * i + 8, :].astype(F32)
+    live = jnp.where(diagonal[None], live[:, None, :], 0.0).reshape(512, 64)
+    live = jnp.sum(live, axis=1, keepdims=True)
     x = sx[rows, :].astype(F32)
     scale = lax.rsqrt(jnp.sum(x * x, axis=1, keepdims=True) / 768.0 + 1e-06)
-    sl = scale * live[:, i : i + 1]
+    sl = scale * live
     sl_out[rows, :] = jnp.broadcast_to(sl, (512, 128))
-    normed[...] = (x * sl * sgain[...]).astype(BF16)
+    normed[...] = (x * sl * sgain[...].reshape(1, 768)).astype(BF16)
 
     def block(n, carry):
         cols = pl.ds(pl.multiple_of(n * 256, 256), 256)
@@ -46,43 +50,47 @@
 
 
 def gather_kernel(
-    tx_hbm, tproj_hbm, tgain, tlive, sx_hbm, sproj_hbm, sgain, slive, pos,
-    ge, gp, praw, sl_out,
-    tx, tproj, sx, sproj, normed,
+    tx_hbm, tproj_hbm, tgain_hbm, tmask_hbm, sx_hbm, sproj_hbm, sgain_hbm, smask_hbm, pos_hbm,
+    ge, gp, praw, sl_out, sgain, sx, sproj,
+    tx, tproj, normed, tgain, tmask, smask, pos,
     sq_own, sq_out, sq_in, sqz_out, sqz_in,
     pe_own, pe_out, pe_in, pez_out, pez_in, T,
-    ld_sem, sq_s, sq_r, pe_s, pe_r, z_s, z_r, a1_s, a1_r, a2_s, a2_r, c_s, c_r,
+    tx_sem, ld_sem, sq_s, sq_r, pe_s, pe_r, z_s, z_r, a1_s, a1_r, a2_s, a2_r, c_s, c_r,
 ):
     zlo, x, zhi, y, core = place()
     z = zhi * 4 + zlo
     two = 2 - 4 * core
 
     def dev(zz, xx, yy, cc):
-        zz, xx, yy = lax.rem(zz + 8, 8), lax.rem(xx + 4, 4), lax.rem(yy + 4, 4)
-        return {"dp": lax.rem(zz, 4) * 4 + xx, "mp": lax.div(zz, 4) * 8 + yy * 2 + cc}
+        zz, xx, yy = (zz + 8) & 7, xx & 3, yy & 3
+        return {"dp": (zz & 3) * 4 + xx, "mp": (zz >> 2) * 8 + yy * 2 + cc}
 
     loads = []
-    for k in range(4):
-        loads.append(pltpu.make_async_copy(tx_hbm.at[pl.ds(16 * k, 16)], tx.at[pl.ds(16 * k, 16)], ld_sem.at[k]))
+    for k in range(8):
+        part = pl.ds(32 * (k // 4) + 16 * (k % 2) + 8 * (k // 2 % 2), 8)
+        loads.append(pltpu.make_async_copy(tx_hbm.at[part], tx.at[part], tx_sem.at[k]))
     loads.append(pltpu.make_async_copy(sx_hbm, sx, ld_sem.at[4]))
     loads.append(pltpu.make_async_copy(sproj_hbm, sproj, ld_sem.at[5]))
     loads.append(pltpu.make_async_copy(tproj_hbm, tproj, ld_sem.at[6]))
-    for c in loads:
+    loads.append(pltpu.make_async_copy(sgain_hbm, sgain, ld_sem.at[7]))
+    loads.append(pltpu.make_async_copy(smask_hbm, smask, ld_sem.at[8]))
+    loads.append(pltpu.make_async_copy(tgain_hbm, tgain, ld_sem.at[9]))
+    loads.append(pltpu.make_async_copy(tmask_hbm, tmask, ld_sem.at[10]))
+    loads.append(pltpu.make_async_copy(pos_hbm, pos, ld_sem.at[11]))
+    for c in loads[:8]:
         c.start()
 
-    peers = []
+    peers = [dev(z, x, y + dy, cc) for dy in range(4) for cc in (core, 1 - core)][1:]
+    peers.append(dev(z + 4, x, y, core))
     for dz in (0, 1, -1, 2, -2):
         for dy in range(4):
-            if (dz, dy) != (0, 0):
+            if dz:
                 peers.append(dev(z + dz, x, y + dy, core))
         for dx in range(1, 4):
             peers.append(dev(z + dz, x + dx, y, core))
     for dx in range(1, 4):
         for dy in range(1, 4):
             peers.append(dev(z, x + dx, y + dy, core))
-    for dy in range(4):
-        peers.append(dev(z, x, y + dy, 1 - core))
-    peers.append(dev(z + 4, x, y, core))
     barrier = pltpu.get_barrier_semaphore()
     for p in peers:
         pl.semaphore_signal(barrier, inc=1, device_id=p, device_id_type=MESH)
@@ -93,20 +101,27 @@
         )
 
     me = y * 2 + core
-    others = [lax.rem(me + k, 8) for k in range(1, 8)]
+    others = [(me + k) & 7 for k in range(1, 8)]
     sends = []
 
     def peer8(s):
-        return dev(z, x, lax.div(s, 2), lax.rem(s, 2))
+        return dev(z, x, s >> 1, s & 1)
+
+    def pair(h, q):
+        p = 32 * h + q
+        return jnp.concatenate([tx[p], tx[p + 16]], axis=0)
 
     row = lax.broadcasted_iota(jnp.int32, (16, 256), 0)
     for h in range(2):
         total = jnp.zeros((16, 256), F32)
         for q in range(16):
             if q % 8 == 0:
-                loads[2 * h + q // 8].wait()
-            p = 32 * h + 2 * q
-            v = tx[p : p + 2].reshape(256, 256)
+                loads[4 * h + 2 * (q // 8)].wait()
+                loads[4 * h + 2 * (q // 8) + 1].wait()
+                if h == 0 and q == 8:
+                    for c in loads[8:]:
+                        c.start()
+            v = pair(h, q)
             pick = jnp.where(row == q, 1.0, 0.0).astype(BF16)
             total = total + lax.dot_general(pick, v * v, NT, preferred_element_type=F32)
         sq_own[h] = total
@@ -118,10 +133,10 @@
             c.start()
             sends.append(c)
 
-    loads[4].wait()
-    loads[5].wait()
+    for k in (8, 9, 11, 12):
+        loads[k].wait()
     student = functools.partial(
-        student_chunk, sx=sx, sproj=sproj, sgain=sgain, live=slive, gp=gp, praw=praw, sl_out=sl_out, normed=normed
+        student_chunk, sx=sx, sproj=sproj, sgain=sgain, mask=smask, gp=gp, praw=praw, sl_out=sl_out, normed=normed
     )
     student(0)
 
@@ -140,27 +155,29 @@
     student(1)
     zc.wait_recv()
 
-    loads[6].wait()
-    row = lax.broadcasted_iota(jnp.int32, (16, 256), 0)
-    lane = lax.broadcasted_iota(jnp.int32, (16, 256), 1)
+    for k in (10, 13, 14, 15):
+        loads[k].wait()
+    row = lax.broadcasted_iota(jnp.int32, (32, 256), 0)
+    lane = lax.broadcasted_iota(jnp.int32, (32, 256), 1)
     pooled = []
     for h in range(2):
         squares = sq_own[h] + sqz_in[h].astype(F32)
-        weight = tlive[16 * h : 16 * h + 16, :] * lax.rsqrt(squares / D + 1e-06)
+        live = jnp.concatenate([tmask[32 * h : 32 * h + 16, :], tmask[32 * h + 16 : 32 * h + 32, :]], axis=1)
+        weight = live.astype(F32) * lax.rsqrt(squares / D + 1e-06)
         high = weight.astype(BF16).astype(F32)
         low = weight - high
-        for g in range(4):
-            total = jnp.zeros((16, 256), F32)
-            for k in range(4):
-                q = 4 * g + k
-                both = jnp.where(row < 8, high[q : q + 1, :], low[q : q + 1, :])
-                mine = lax.rem(row, 8) == 2 * k + lax.div(lane, 128)
+        halves = []
+        for g in range(2):
+            total = jnp.zeros((32, 256), F32)
+            for k in range(8):
+                q = 8 * g + k
+                both = jnp.where(row < 16, high[q : q + 1, :], low[q : q + 1, :])
+                mine = (row & 15) == k + 8 * (lane >> 7)
                 lhs = jnp.where(mine, both, 0.0).astype(BF16)
-                p = 32 * h + 2 * q
-                v = tx[p : p + 2].reshape(256, 256)
-                total = total + jnp.dot(lhs, v, preferred_element_type=F32)
-            pooled.append(total[:8] + total[8:])
-    tpooled = (jnp.concatenate(pooled, axis=0) * tgain[...]).astype(BF16)
+                total = total + jnp.dot(lhs, pair(h, q), preferred_element_type=F32)
+            halves.append(total[:16] + total[16:])
+        pooled += [halves[0][:8], halves[1][:8], halves[0][8:], halves[1][8:]]
+    tpooled = (jnp.concatenate(pooled, axis=0) * tgain[...].reshape(1, 256)).astype(BF16)
     partial = jnp.dot(tpooled, tproj[...], preferred_element_type=F32).reshape(8, 8, 1024)
     pe_own[...] = partial
     pe_out[...] = partial.astype(BF16)
@@ -185,7 +202,7 @@
     T[core, zlo, x, y] = (traw * scale / 32.0).astype(BF16)
 
     zoffs = (0, 1, -1, two)
-    ahead = lambda v, k: lax.rem(v + k, 4)
+    ahead = lambda v, k: (v + k) & 3
 
     def plane(part, az, ax, ay):
         lo, n = PARTS[part]
@@ -220,7 +237,7 @@
     for part in range(3):
         mine = plane(part, zlo, x, y)
         for k in range(1, 16):
-            s = lax.rem(slots[part] + k, 16)
+            s = (slots[part] + k) & 15
             remote(mine, mine, a1_s.at[part, k - 1], a1_r.at[part, s], other).wait_recv()
         v = own_line[part]
         src = line(part, core, v)
@@ -254,7 +271,10 @@
     semb = praws * lax.rsqrt(jnp.mean(praws * praws, axis=-1, keepdims=True) + 1e-06) / 32.0
     temb = T[...].reshape(1024, 1024)
     lanes = lax.broadcasted_iota(jnp.int32, (32, 1024), 1)
-    picker = jnp.where(pos[...] == lanes, 1.0, 0.0).astype(BF16)
+    diagonal = lax.broadcasted_iota(jnp.int32, (32, 32), 0) == lax.broadcasted_iota(jnp.int32, (32, 32), 1)
+    wanted = jnp.sum(jnp.where(diagonal, pos[...].reshape(1, 32), 0), axis=1, keepdims=True)
+    wanted = ((wanted >> 3) & 1) * 512 + (wanted >> 8) * 128 + ((wanted >> 6) & 3) * 32 + ((wanted >> 4) & 3) * 8 + (wanted & 7)
+    picker = jnp.where(wanted == lanes, 1.0, 0.0).astype(BF16)
     tpos = jnp.dot(picker, temb, preferred_element_type=F32).astype(BF16)
     both = jnp.concatenate([tpos, semb.astype(BF16)], axis=0)
     logits = lax.dot_general(both, temb, NT, preferred_element_type=F32)
@@ -273,7 +293,7 @@
     p, g = praw[...], ge[...]
     r = lax.rsqrt(jnp.mean(p * p, axis=-1, keepdims=True) + 1e-06)
     ds = (g * r - p * (r * r * r) * jnp.mean(p * g, axis=-1, keepdims=True)) / 32.0
-    gain = sgain[...]
+    gain = sgain[...].reshape(1, 768)
     for i in range(8):
         rows = pl.ds(256 * i, 256)
         slope = gp[rows, :].astype(F32).reshape(4, 64, 1024)
@@ -298,13 +318,7 @@
     hbm = pl.BlockSpec(memory_space=pltpu.HBM)
     dma = pltpu.SemaphoreType.DMA
     in_hbm = lambda a: pltpu.with_memory_space_constraint(a, pltpu.HBM)
-    sx = student_states.reshape(2048, 768)
-    sgain = student_gain.reshape(1, 768)
-    slive = student_mask.astype(F32).reshape(4, 512).T
-    tlive = teacher_mask.astype(F32).reshape(32, 256)
-    p = positive
-    pos = ((p // 8) % 2) * 512 + (p // 256) * 128 + ((p // 64) % 4) * 32 + ((p // 16) % 4) * 8 + p % 8
-    ge, gp, praw, sl = pl.pallas_call(
+    ge, gp, praw, sl, sgain, sx, sproj = pl.pallas_call(
         gather_kernel,
         name="gather",
         out_shape=(
@@ -312,15 +326,20 @@
             jax.ShapeDtypeStruct((2048, 1024), BF16),
             jax.ShapeDtypeStruct((32, 1024), F32),
             jax.ShapeDtypeStruct((2048, 128), F32),
+            jax.ShapeDtypeStruct((768,), F32),
+            jax.ShapeDtypeStruct((2048, 768), BF16),
+            jax.ShapeDtypeStruct((768, 1024), BF16),
         ),
-        in_specs=[hbm, hbm, vmem, vmem, hbm, hbm, vmem, vmem, vmem],
-        out_specs=(vmem, vmem, vmem, vmem),
+        in_specs=[hbm] * 9,
+        out_specs=(vmem,) * 7,
         scratch_shapes=[
             pltpu.VMEM((64, 128, 256), BF16),
             pltpu.VMEM((256, 1024), BF16),
-            pltpu.VMEM((2048, 768), BF16),
-            pltpu.VMEM((768, 1024), BF16),
             pltpu.VMEM((512, 768), BF16),
+            pltpu.VMEM((256,), F32),
+            pltpu.VMEM((64, 128), jnp.int32),
+            pltpu.VMEM((32, 64), jnp.int32),
+            pltpu.VMEM((32,), jnp.int32),
             pltpu.VMEM((2, 16, 256), F32),
             pltpu.VMEM((2, 16, 256), BF16),
             pltpu.VMEM((2, 8, 16, 256), BF16),
@@ -332,15 +351,17 @@
             pltpu.VMEM((8, 1024), BF16),
             pltpu.VMEM((8, 1024), BF16),
             pltpu.VMEM((2, 4, 4, 4, 8, 1024), BF16),
-            dma((7,)), dma((2, 8)), dma((2, 8)), dma((8,)), dma((8,)), dma((2,)), dma((2,)),
+            dma((8,)), dma((12,)), dma((2, 8)), dma((2, 8)), dma((8,)), dma((8,)), dma((2,)), dma((2,)),
             dma((3, 15)), dma((3, 16)), dma((3, 3)), dma((3, 4)), dma((3, 4)), dma((3, 4)),
         ],
         compiler_params=pltpu.CompilerParams(
             collective_id=0, has_side_effects=True, vmem_limit_bytes=36 * 2**20
         ),
     )(
-        in_hbm(teacher_states), in_hbm(teacher_proj), teacher_gain.reshape(1, 256), tlive,
-        in_hbm(sx), in_hbm(student_proj), sgain, slive, pos.reshape(32, 1),
+        *map(in_hbm, (
+            teacher_states, teacher_proj, teacher_gain, teacher_mask,
+            student_states.reshape(2048, 768), student_proj, student_gain, student_mask, positive,
+        )),
     )
     grad_embed, grad_states = pl.pallas_call(
         back_kernel,
@@ -350,7 +371,7 @@
         out_specs=(hbm, hbm),
         scratch_shapes=[pltpu.VMEM((2048, 768), BF16), dma((9,))],
         compiler_params=pltpu.CompilerParams(vmem_limit_bytes=36 * 2**20),
-    )(ge, praw, gp, sl, student_proj, sgain, sx)
+    )(ge, praw, gp, sl, sproj, sgain, sx)
     return grad_embed, grad_states.reshape(32, 64, 768)
 
 

time: 56.8 us -> 52.9 us (0.931)
  other arithmetic: 2.16 us -> 0 us
  local copies, waits for them, and re-layouts: 1.7 us -> 0 us
    convert_element_type x2 -> x0, other arithmetic: 1.48 us -> none  [the longest x1 0.76 us: shards(): tlive = teacher_mask.astype(F32).reshape(32, 256)]
    reshape x5 -> x0, local copies, waits for them, and re-layouts: 1.02 us -> none  [the longest x1 0.69 us: shards(): sgain = student_gain.reshape(1, 768)]
    unnamed x6 -> x0, local copies, waits for them, and re-layouts: 0.69 us -> none
    reshape x1 -> x0, other arithmetic: 0.68 us -> none  [shards(): pos.reshape(32, 1)]
where the time goes in v2:
time: 52.9 us; the launch traced here: 52.8 us
  Pallas kernels  52.2 us (99%)
  between operations  0.64 us (1%)
    pallas_call x1, Pallas kernels, shards(): pl.pallas_call(gather_kernel, name='gather', out_shape=(jax.ShapeDtypeStr...  46.5 us
    pallas_call x1, Pallas kernels, shards(): pl.pallas_call(back_kernel, name='back', out_shape=(jax.ShapeDtypeStruct(...  5.68 us

profile of v2, /device:TPU:1, one launch (start us, length us, event | category | flops | bytes accessed | tf_op | source)
XLA Modules:
  0.0 52.8 jit_solution(8600557391207709014)
XLA Ops:
  0.6 46.5 %gather.1 = (f32[32,1024]{1,0:T(8,128)S(1)}, bf16[2048,1024]{1,0:T(8,128)(2,1)S(1)}, f32[32,1024]{1,0:T(8,128)S(1)}, f32[2048,128]{1,0:T(8,128)S(1)}, f32[768]{0...) custom-call(bf16[64,128,256]{2,1,0:T(8,128)(2,1)} %tx_hbm.1, bf16[256,1024]{1,0:T(8,128)(2,1)} %tproj_hbm.1, ...), custom_call_target="tpu_custom_call" | custom-call | tf_op jit(solution)/shard_map/gather/pallas_call | solution.py:321
  47.2 5.7 %back.1 = (f32[32,1024]{1,0:T(8,128)}, bf16[2048,768]{1,0:T(8,128)(2,1)}) custom-call(f32[32,1024]{1,0:T(8,128)S(1)} %get-tuple-element.11.ge, f32[32,1024]{1,0:T(8,128)S(1)} %get-tuple-element.12.praw, bf16[2048,1024]{1,0:T(8,128)(2,1)S(1)} %get-tuple-element.13.gp, f32[2048,128]{1,0:T(8,128)S(1)} %get-tuple-element.14.sl_in, ...), custom_call_target="tpu_custom_call" | custom-call | tf_op jit(solution)/shard_map/back/pallas_call | solution.py:366
